TPU v7x, 32 devices: a whole 2x2x4 slice. The times are simulated.
32 devices in a mesh: groups: 2 (over x), row: 8 (over z, y), head: 2 (over core).
Axes of the slice: x: 2, y: 2, z: 4, core: 2. Of those that a mesh axis runs over, the one named last changes fastest.
Arguments:
- hidden: bfloat16 [48, 4096], P('groups'), parts along dimension 0, may hold values from -6 to 6
- norm_gain: float32 [4096], replicated, may hold values from 0.1 to 1.9
- w_query: bfloat16 [8, 256, 4096], P('head', 'row'), may hold values from -0.09375 to 0.09375
- w_key: bfloat16 [8, 256, 4096], P('head', 'row'), may hold values from -0.09375 to 0.09375
- w_value: bfloat16 [8, 512, 4096], P('head', 'row'), may hold values from -0.09375 to 0.09375
- w_outgate: bfloat16 [8, 512, 4096], P('head', 'row'), may hold values from -0.09375 to 0.09375
- w_out: bfloat16 [8, 512, 4096], P('head', 'row'), may hold values from -0.125 to 0.125
- w_gates: bfloat16 [2, 8, 4096], P(None, 'head'), may hold values from -0.09375 to 0.09375
- gate_bias: float32 [2, 8], P(None, 'head'), may hold values from -2 to 4
- headnorm_gain: float32 [8, 512], P('head', 'row'), may hold values from 0.1 to 1.9
- final_gain: float32 [4096], replicated, may hold values from 0.1 to 1.9
- w_vocab: bfloat16 [25152, 4096], P(('row', 'head')), may hold values from -39.0625 to 39.0625
- memory: float32 [48, 8, 256, 512], P('groups', 'head', 'row'), parts along dimension 0, may hold values from -6 to 6
- normalizer: float32 [48, 8, 256], P('groups', 'head', 'row'), parts along dimension 0, may hold values from -6 to 6
- stabilizer: float32 [48, 8], P('groups', 'head'), parts along dimension 0, may hold values from -2 to 2
- targets: int32 [48], P('groups'), parts along dimension 0, may hold values from 0 to 25151
Outputs:
- memory_out: float32 [48, 8, 256, 512], P('groups', 'head', 'row'), parts along dimension 0
- normalizer_out: float32 [48, 8, 256], P('groups', 'head', 'row'), parts along dimension 0
- stabilizer_out: float32 [48, 8], P('groups', 'head'), parts along dimension 0
- hidden_out: bfloat16 [48, 4096], P('groups', ('row', 'head')), parts along dimension 0
- log_prob: float32 [48], P('groups'), parts along dimension 0
There are 2 independent parts, one for each index of `groups`. A program takes and returns all parts, laid end to end along the dimension named above; an argument that names none is the same for every part. Nothing has to cross between parts.
All inputs are finite; a program needn't handle non-finite values.
Results may differ from a plain program's by a relative error of at most 0.0035.
The roundings to bfloat16 on the way count: a program that leaves them out, or rounds other values in their place, can miss the bound.
Values may be sent and summed in bfloat16 or wider, within the bound.
A program may use at most 64 MiB of HBM per device.

v0:
```python
import math
import jax
import jax.numpy as jnp
from jax import lax
from jax.sharding import PartitionSpec as P

QK_DIM = 256
epsilon = 1e-06


def joined_2(value, axis, join):
    pieces = jax.tree.map(lambda part: lax.all_gather(part, axis), value)
    head = jax.tree.map(lambda part: part[0], pieces)
    tail = jax.tree.map(lambda part: part[1:], pieces)
    total, _ = lax.scan(lambda total, share: (join(total, share), None), head, tail)
    return total


def rms_round(stream, gain):
    scale = lax.rsqrt(jnp.mean(stream * stream, axis=-1, keepdims=True) + epsilon)
    return (stream * scale * gain).astype(jnp.bfloat16)


def per_device(
    hidden,
    norm_gain,
    w_query,
    w_key,
    w_value,
    w_outgate,
    w_out,
    w_gates,
    gate_bias,
    headnorm_gain,
    final_gain,
    w_vocab,
    memory,
    normalizer,
    stabilizer,
    targets,
):
    value_rows = w_value.shape[1]
    stream = hidden.astype(jnp.float32)
    normed_in = rms_round(stream, norm_gain)

    def project(weights):
        return jnp.einsum("sd,hjd->shj", normed_in, weights, preferred_element_type=jnp.float32)

    queries = project(w_query) / math.sqrt(QK_DIM)
    key_part = project(w_key)
    value_part = project(w_value).astype(jnp.bfloat16)
    outgate_pre = project(w_outgate)
    gate_pre = (
        jnp.einsum("sd,ghd->gsh", normed_in, w_gates, preferred_element_type=jnp.float32)
        + gate_bias[:, None, :]
    )
    log_forget = jax.nn.log_sigmoid(gate_pre[1])
    stabilizer_out = jnp.maximum(log_forget + stabilizer, gate_pre[0])
    decay_rate = jnp.exp(log_forget + stabilizer - stabilizer_out)
    inflow = jnp.exp(gate_pre[0] - stabilizer_out)
    scaled_key = inflow[:, :, None] * key_part
    memory_out = (
        decay_rate[:, :, None, None] * memory
        + scaled_key[:, :, :, None]
        * lax.all_gather(value_part, "row", axis=2, tiled=True).astype(jnp.float32)[:, :, None, :]
    )
    normalizer_out = decay_rate[:, :, None] * normalizer + scaled_key
    partial_readout = jnp.einsum(
        "shj,shje->she", queries, memory_out, precision=lax.Precision.HIGHEST
    )
    readout = lax.psum(partial_readout, "row")
    average = jnp.mean(readout, axis=-1)
    centered_full = readout - average[:, :, None]
    variance = jnp.mean(centered_full * centered_full, axis=-1)
    centered = lax.dynamic_slice_in_dim(
        centered_full, lax.axis_index("row") * value_rows, value_rows, 2
    )
    normed = centered * lax.rsqrt(variance + epsilon)[:, :, None] * headnorm_gain
    gated_out = (jax.nn.sigmoid(outgate_pre) * normed).astype(jnp.bfloat16)
    partial_terms = jnp.einsum("shj,hjd->sd", gated_out, w_out, preferred_element_type=jnp.float32)
    position = lax.axis_index("row") * lax.axis_size("head") + lax.axis_index("head")
    share_width = hidden.shape[1] // (lax.axis_size("row") * lax.axis_size("head"))
    vocab_here = w_vocab.shape[0]
    projection = lax.psum(partial_terms, ("row", "head"))
    new_full = (stream + projection).astype(jnp.bfloat16)
    final_feat = rms_round(new_full.astype(jnp.float32), final_gain)
    logits = jnp.einsum("sd,vd->sv", final_feat, w_vocab, preferred_element_type=jnp.float32)
    hidden_out = lax.dynamic_slice_in_dim(new_full, position * share_width, share_width, 1)
    local_ids = targets - position * vocab_here
    is_target = jnp.arange(vocab_here, dtype=jnp.int32)[None, :] == local_ids[:, None]
    target_term = jnp.sum(jnp.where(is_target, logits, 0.0), axis=-1)
    local_max = jnp.max(logits, axis=-1)
    local_sum = jnp.sum(jnp.exp(logits - local_max[:, None]), axis=-1)

    def combine(earlier, later):
        highest = jnp.maximum(earlier[0], later[0])
        joined = earlier[1] * jnp.exp(earlier[0] - highest) + later[1] * jnp.exp(later[0] - highest)
        return (highest, joined, earlier[2] + later[2])

    highest, exp_total, picked = joined_2(
        (local_max, local_sum, target_term), ("row", "head"), combine
    )
    log_prob = picked - (highest + jnp.log(exp_total))
    return (memory_out, normalizer_out, stabilizer_out, hidden_out, log_prob)


def solution(mesh):
    in_specs = (
        P("groups", None),
        P(),
        P("head", "row", None),
        P("head", "row", None),
        P("head", "row", None),
        P("head", "row", None),
        P("head", "row", None),
        P(None, "head", None),
        P(None, "head"),
        P("head", "row"),
        P(),
        P(("row", "head"), None),
        P("groups", "head", "row", None),
        P("groups", "head", "row"),
        P("groups", "head"),
        P("groups"),
    )
    out_specs = (
        P("groups", "head", "row", None),
        P("groups", "head", "row"),
        P("groups", "head"),
        P("groups", ("row", "head")),
        P("groups"),
    )
    return jax.shard_map(
        per_device, mesh=mesh, in_specs=in_specs, out_specs=out_specs, check_vma=False
    )
```

profile of v0, /device:TPU:0, one launch (start us, length us, event | category | flops | bytes accessed | tf_op | source)
XLA Modules:
  0.0 280.0 jit_solution(1592682969917463788)
XLA Ops:
  7.2 1.2 fusion.17
  8.5 2.7 convolution_convert_fusion
  11.3 33.0 %all_gather.21 = bf16[24,4,512]{0,1,2:T(4,128)(2,1)S(1)} all-gather(bf16[24,4,64]{0,1,2:T(4,128)(2,1)S(1)} %copy.34), channel_id=1, replica_groups=mesh['groups'=2,'row'=8,'head'=2] {'row'}, dimensions={2}, use_global_device_ids=true | all-gather | bytes 110592 | tf_op jit(solution)/shard_map/all_gather | solution.py:65
  44.7 1.2 fusion.13
  45.9 0.7 subtract_exponential_fusion.1
  46.7 2.2 fusion.28
  48.9 2.2 fusion.7
  51.1 3.4 %multiply_add_fusion = f32[24,4,32,512]{3,2,1,0:T(8,128)S(1)} fusion(f32[24,4,32,512]{3,2,1,0:T(8,128)} %param.30, f32[24,4,512]{2,1,0:T(4,128)S(1)} %copy.36, f32[24,4,32]{2,1,0:T(4,128)S(1)} %copy.33, f32[24,4]{1,0:T(8,128)S(1)} %copy.32), kind=kLoop, calls=%fused_computation.10 | loop fusion | flops 4718592 | bytes 12792192 | tf_op jit(solution)/shard_map/add | solution.py:63
  54.5 2.7 copy-done.1
  57.2 3.1 %fusion.26 = f32[24,4,1,512]{3,2,1,0:T(1,128)S(1)} fusion(f32[24,4,32,512]{3,2,1,0:T(8,128)S(1)} %multiply_add_fusion, f32[24,4,32,1]{2,0,1,3:T(8,128)S(1)} %fusion.7), kind=kOutput, calls=%fused_computation.46 | convolution fusion | flops 18874368 | bytes 6500352 | tf_op jit(solution)/shard_map/shj,shje->she/dot_general | solution.py:68
  60.4 0.7 copy.47
  61.2 0.6 copy.38
  61.8 0.6 dynamic-slice
  63.1 70.0 %all-reduce.7.cloned.1.call-done = f32[24,4,512]{2,0,1:T(8,128)} async-done(((f32[24,4,512]{2,0,1:T(8,128)}), f32[24,4,512]{2,0,1:T(8,128)}) %all-reduce.7.cloned.1.call-update) | async-done | bytes 196624 | tf_op jit(solution)/shard_map/psum | solution.py:71
  133.1 1.0 reduce_sum.55
  134.1 1.1 multiply_reduce_fusion
  135.3 3.8 %convolution_bitcast_fusion = f32[24,4096]{1,0:T(8,128)} fusion(bf16[4,64,4096]{2,1,0:T(8,128)(2,1)S(1)} %copy-done, bf16[4,64,4096]{2,1,0:T(8,128)(2,1)} %param.23, f32[24,4,512]{2,0,1:T(8,128)S(1)} %get-tuple-element.86, s32[]{:T(128)S(6)} %select_n.16, f32[4,64]{1,0:T(4,128)S(1)} %copy-done.6, f32[24,4]{0,1:T(4,128)S(1)} %add_rsqrt_fusion, ...), kind=kOutput, calls=%fused_computation.11 | convolution fusion | flops 101099520 | bytes 4854276 | tf_op jit(solution)/shard_map/shj,hjd->sd/dot_general | solution.py:80
  139.1 90.6 %all-reduce.9.cloned.1.call-done = f32[24,4096]{1,0:T(8,128)} async-done(((f32[24,4096]{1,0:T(8,128)}), f32[24,4096]{1,0:T(8,128)}) %all-reduce.9.cloned.1.call-update) | async-done | bytes 393232 | tf_op jit(solution)/shard_map/psum | solution.py:84
  229.6 1.2 fusion.14
  230.8 8.3 %fusion.50 = (f32[24]{0:T(128)S(1)}, f32[24,1572]{1,0:T(8,128)S(1)}) fusion(bf16[1572,4096]{1,0:T(8,128)(2,1)} %param.29, bf16[24,4096]{1,0:T(8,128)(2,1)S(1)} %get-tuple-element.84, f32[4096]{0:T(1024)S(1)} %copy-done.4, f32[24]{0:T(128)S(1)} %add_rsqrt_fusion.1), kind=kOutput, calls=%fused_computation.74 | convolution fusion | flops 309498688 | bytes 13241920 | tf_op jit(solution)/shard_map/sd,vd->sv/dot_general | solution.py:87
  240.0 30.9 %all-reduce.3 = (f32[384]{0:T(512)S(1)}, f32[384]{0:T(512)S(1)}, f32[384]{0:T(512)S(1)}) all-reduce(f32[384]{0:T(512)S(1)} %dynamic-update-slice, f32[384]{0:T(512)S(1)} %dynamic-update-slice.1, f32[384]{0:T(512)S(1)} %dynamic-update-slice.2), channel_id=2, replica_groups=mesh['groups'=2,'row'=8,'head'=2] {'row','head'}, use_global_device_ids=true, to_apply=%add | all-reduce | flops 1152 | bytes 9216
  271.2 0.6 constant_dynamic-slice_fusion.3
  272.0 0.6 while.14
  272.7 0.5 add_subtract_fusion
  (63 shorter events, 2.6 us)
Async XLA Ops:
  7.2 128.1 %copy-start = (bf16[4,64,4096]{2,1,0:T(8,128)(2,1)S(1)}, bf16[4,64,4096]{2,1,0:T(8,128)(2,1)}, u32[]{:S(2)}) copy-start(bf16[4,64,4096]{2,1,0:T(8,128)(2,1)} %param.24) | copy-start | bytes 6291460
  7.2 125.9 %all-reduce.7.cloned.1.call-start = ((), (), s32[]{:S(2)}) async-start(), calls=%async_computation | async-start | bytes 393216 | tf_op jit(solution)/shard_map/psum | solution.py:71
  46.6 7.9 %copy-start.5 = (f32[24,4]{0,1:T(4,128)}, f32[24,4]{0,1:T(4,128)S(1)}, u32[]{:S(2)}) copy-start(f32[24,4]{0,1:T(4,128)S(1)} %get-tuple-element.88) | copy-start | bytes 1156
  54.5 2.7 copy-start.1
  57.2 4.6 %copy-start.8 = (u32[32]{0:T(128)S(1)}, u32[32]{0:T(128)}, u32[]{:S(2)}) copy-start(u32[32]{0:T(128)} %constant.57) | copy-start | bytes 388
  57.2 78.0 %copy-start.2 = (bf16[24,4096]{1,0:T(8,128)(2,1)S(1)}, bf16[24,4096]{1,0:T(8,128)(2,1)}, u32[]{:S(2)}) copy-start(bf16[24,4096]{1,0:T(8,128)(2,1)} %param.18) | copy-start | bytes 589828
  57.2 78.0 %copy-start.3 = (f32[4096]{0:T(1024)S(1)}, f32[4096]{0:T(1024)}, u32[]{:S(2)}) copy-start(f32[4096]{0:T(1024)} %param.19) | copy-start | bytes 49156
  57.2 78.1 %copy-start.6 = (f32[4,64]{1,0:T(4,128)S(1)}, f32[4,64]{1,0:T(4,128)}, u32[]{:S(2)}) copy-start(f32[4,64]{1,0:T(4,128)} %param.27) | copy-start | bytes 3076
  57.2 81.8 %copy-start.7 = (s32[24]{0:T(128)S(1)}, s32[24]{0:T(128)}, u32[]{:S(2)}) copy-start(s32[24]{0:T(128)} %param.33) | copy-start | bytes 292
  57.2 173.6 %copy-start.4 = (f32[4096]{0:T(1024)S(1)}, f32[4096]{0:T(1024)}, u32[]{:S(2)}) copy-start(f32[4096]{0:T(1024)} %param.28) | copy-start | bytes 49156
  61.1 168.5 %all-reduce.9.cloned.1.call-start = ((), (), s32[]{:S(2)}) async-start(), calls=%async_computation.1 | async-start | bytes 786432 | tf_op jit(solution)/shard_map/psum | solution.py:84
Sparse Core Ops, SparseCore 0:
  61.2 71.7 all-reduce.6
  139.2 90.4 all-reduce.8
where the time goes:
time: 281 us; the launch traced here: 280 us
  waiting for transfers between devices  161 us (57%)
  blocking collectives  64 us (23%)
  matrix products  23.4 us (8%)
  between operations  15 us (5%)
  other arithmetic  9.78 us (3%)
  local copies, waits for them, and re-layouts  7.02 us (2%)
    psum x1, waiting for transfers between devices, per_device(): projection = lax.psum(partial_terms, ('row', 'head'))  90.6 us
    psum x1, waiting for transfers between devices, per_device(): readout = lax.psum(partial_readout, 'row')  70 us
    all_gather x1, blocking collectives, per_device(): lax.all_gather(value_part, 'row', axis=2, tiled=True).astype(jnp.float32)  33 us
    unnamed x1, blocking collectives  30.9 us
    dot_general x1, matrix products, per_device(): jnp.einsum('sd,vd->sv', final_feat, w_vocab, preferred_element_type=jnp.f...  8.26 us
    dot_general x3, matrix products, project(): jnp.einsum('sd,hjd->shj', normed_in, weights, preferred_element_type=jnp....  7.03 us
  transfers between devices with their start and end apart: 2, of which 2 were waited for; matrix products, arithmetic and copies ran while one was open for 0% of the time, Pallas kernels for 0%

commit v1 on v0

--- a/solution.py
+++ b/solution.py
@@ -81,7 +81,7 @@
     position = lax.axis_index("row") * lax.axis_size("head") + lax.axis_index("head")
     share_width = hidden.shape[1] // (lax.axis_size("row") * lax.axis_size("head"))
     vocab_here = w_vocab.shape[0]
-    projection = lax.psum(partial_terms, ("row", "head"))
+    projection = jnp.sum(lax.all_gather(partial_terms, ("row", "head")), axis=0)
     new_full = (stream + projection).astype(jnp.bfloat16)
     final_feat = rms_round(new_full.astype(jnp.float32), final_gain)
     logits = jnp.einsum("sd,vd->sv", final_feat, w_vocab, preferred_element_type=jnp.float32)

time: 281 us -> 254 us (0.904)
  waiting for transfers between devices: 161 us -> 131 us
    psum x1 -> x0, waiting for transfers between devices: 90.6 us -> none  [per_device(): projection = lax.psum(partial_terms, ('row', 'head'))]
    all_gather x0 -> x1, waiting for transfers between devices: none -> 58.7 us  [per_device(): projection = jnp.sum(lax.all_gather(partial_terms, ('row', 'head')), axis=0)]
    reduce_sum x0 -> x1, other arithmetic: none -> 3.11 us  [per_device(): projection = jnp.sum(lax.all_gather(partial_terms, ('row', 'head')), axis=0)]
where the time goes in v1:
time: 254 us; the launch traced here: 253 us
  waiting for transfers between devices  131 us (52%)
  blocking collectives  64.9 us (26%)
  matrix products  23.4 us (9%)
  between operations  15 us (6%)
  other arithmetic  11.9 us (5%)
  local copies, waits for them, and re-layouts  7.02 us (3%)
    psum x1, waiting for transfers between devices, per_device(): readout = lax.psum(partial_readout, 'row')  71.9 us
    all_gather x1, waiting for transfers between devices, per_device(): projection = jnp.sum(lax.all_gather(partial_terms, ('row', 'head')), axis=0)  58.7 us
    all_gather x1, blocking collectives, per_device(): lax.all_gather(value_part, 'row', axis=2, tiled=True).astype(jnp.float32)  33 us
    unnamed x1, blocking collectives  31.8 us
    dot_general x1, matrix products, per_device(): jnp.einsum('sd,vd->sv', final_feat, w_vocab, preferred_element_type=jnp.f...  8.26 us
    dot_general x3, matrix products, project(): jnp.einsum('sd,hjd->shj', normed_in, weights, preferred_element_type=jnp....  7.03 us
  transfers between devices with their start and end apart: 2, of which 2 were waited for; matrix products, arithmetic and copies ran while one was open for 0% of the time, Pallas kernels for 0%

profile of v1, /device:TPU:0, one launch (start us, length us, event | category | flops | bytes accessed | tf_op | source)
XLA Modules:
  0.0 253.1 jit_solution(13840420870915833634)
XLA Ops:
  7.2 1.2 fusion.17
  8.5 2.7 %convolution_convert_fusion = bf16[24,4,64]{2,0,1:T(8,128)(2,1)S(1)} fusion(bf16[4,64,4096]{2,1,0:T(8,128)(2,1)} %param.22, bf16[24,4096]{1,0:T(8,128)(2,1)} %param.18, f32[4096]{0:T(1024)} %param.19, f32[24]{0:T(128)S(1)} %add_rsqrt_fusion.2), kind=kOutput, calls=%fused_computation.21 | convolution fusion | flops 50731008 | bytes 2322528 | tf_op jit(solution)/shard_map/sd,hjd->shj/dot_general | solution.py:47
  11.3 33.0 %all_gather.27 = bf16[24,4,512]{0,1,2:T(4,128)(2,1)S(1)} all-gather(bf16[24,4,64]{0,1,2:T(4,128)(2,1)S(1)} %copy.34), channel_id=1, replica_groups=mesh['groups'=2,'row'=8,'head'=2] {'row'}, dimensions={2}, use_global_device_ids=true | all-gather | bytes 110592 | tf_op jit(solution)/shard_map/all_gather | solution.py:65
  44.7 1.2 fusion.13
  45.9 0.7 subtract_exponential_fusion.1
  46.7 2.2 fusion.28
  48.9 2.2 fusion.7
  51.1 3.4 %multiply_add_fusion = f32[24,4,32,512]{3,2,1,0:T(8,128)S(1)} fusion(f32[24,4,32,512]{3,2,1,0:T(8,128)} %param.30, f32[24,4,512]{2,1,0:T(4,128)S(1)} %copy.36, f32[24,4,32]{2,1,0:T(4,128)S(1)} %copy.33, f32[24,4]{1,0:T(8,128)S(1)} %copy.32), kind=kLoop, calls=%fused_computation.10 | loop fusion | flops 4718592 | bytes 12792192 | tf_op jit(solution)/shard_map/add | solution.py:63
  54.5 2.7 %copy-done.1 = f32[24,4,32,512]{3,2,1,0:T(8,128)} copy-done((f32[24,4,32,512]{3,2,1,0:T(8,128)}, f32[24,4,32,512]{3,2,1,0:T(8,128)S(1)}, u32[]{:S(2)}) %copy-start.1) | copy-done | bytes 6291480
  57.2 3.1 %fusion.26 = f32[24,4,1,512]{3,2,1,0:T(1,128)S(1)} fusion(f32[24,4,32,512]{3,2,1,0:T(8,128)S(1)} %multiply_add_fusion, f32[24,4,32,1]{2,0,1,3:T(8,128)S(1)} %fusion.7), kind=kOutput, calls=%fused_computation.46 | convolution fusion | flops 18874368 | bytes 6500352 | tf_op jit(solution)/shard_map/shj,shje->she/dot_general | solution.py:68
  60.3 0.7 copy.47
  61.2 71.9 %all-reduce.6.cloned.1.call-done = f32[24,4,512]{2,0,1:T(8,128)} async-done(((f32[24,4,512]{2,0,1:T(8,128)}), f32[24,4,512]{2,0,1:T(8,128)}) %all-reduce.6.cloned.1.call-update) | async-done | bytes 196624 | tf_op jit(solution)/shard_map/psum | solution.py:71
  133.1 1.0 reduce_sum.64
  134.1 1.1 multiply_reduce_fusion
  135.3 3.8 %convolution_bitcast_fusion = f32[24,4096]{1,0:T(8,128)} fusion(bf16[4,64,4096]{2,1,0:T(8,128)(2,1)S(1)} %copy-done, bf16[4,64,4096]{2,1,0:T(8,128)(2,1)} %param.23, f32[24,4,512]{2,0,1:T(8,128)S(1)} %get-tuple-element.86, s32[]{:T(128)S(6)} %select_n.16, f32[4,64]{1,0:T(4,128)S(1)} %copy-done.6, f32[24,4]{0,1:T(4,128)S(1)} %add_rsqrt_fusion, ...), kind=kOutput, calls=%fused_computation.11 | convolution fusion | flops 101099520 | bytes 4854276 | tf_op jit(solution)/shard_map/shj,hjd->sd/dot_general | solution.py:80
  139.1 0.6 copy.38
  139.7 0.6 dynamic-slice
  141.0 58.7 %all-gather.6.cloned.1.call-done = f32[384,4096]{1,0:T(8,128)} async-done(((f32[24,4096]{1,0:T(8,128)}), f32[384,4096]{1,0:T(8,128)}) %all-gather.6.cloned.1.call-update) | async-done | bytes 6291472 | tf_op jit(solution)/shard_map/all_gather | solution.py:84
  199.7 3.1 %reduce_sum.66 = f32[24,4096]{1,0:T(8,128)S(1)} reduce(f32[16,24,4096]{2,1,0:T(8,128)} %bitcast.64, f32[]{:T(128)} %constant.14.clone.1), dimensions={0}, to_apply=%region_4.5 | reduce | flops 1474560 | bytes 6684676 | tf_op jit(solution)/shard_map/reduce_sum | solution.py:84
  203.0 8.3 %fusion.50 = (f32[24]{0:T(128)S(1)}, f32[24,1572]{1,0:T(8,128)S(1)}) fusion(bf16[1572,4096]{1,0:T(8,128)(2,1)} %param.29, bf16[24,4096]{1,0:T(8,128)(2,1)S(1)} %get-tuple-element.84, f32[4096]{0:T(1024)S(1)} %copy-done.4, f32[24]{0:T(128)S(1)} %add_rsqrt_fusion.1), kind=kOutput, calls=%fused_computation.74 | convolution fusion | flops 309498688 | bytes 13241920 | tf_op jit(solution)/shard_map/sd,vd->sv/dot_general | solution.py:87
  212.2 31.8 %all-reduce.3 = (f32[384]{0:T(512)S(1)}, f32[384]{0:T(512)S(1)}, f32[384]{0:T(512)S(1)}) all-reduce(f32[384]{0:T(512)S(1)} %dynamic-update-slice, f32[384]{0:T(512)S(1)} %dynamic-update-slice.1, f32[384]{0:T(512)S(1)} %dynamic-update-slice.2), channel_id=3, replica_groups=mesh['groups'=2,'row'=8,'head'=2] {'row','head'}, use_global_device_ids=true, to_apply=%add | all-reduce | flops 1152 | bytes 9216
  244.2 0.6 constant_dynamic-slice_fusion.3
  245.1 0.6 while.14
  245.7 0.5 add_subtract_fusion
  (64 shorter events, 2.7 us)
Async XLA Ops:
  7.2 128.0 %copy-start = (bf16[4,64,4096]{2,1,0:T(8,128)(2,1)S(1)}, bf16[4,64,4096]{2,1,0:T(8,128)(2,1)}, u32[]{:S(2)}) copy-start(bf16[4,64,4096]{2,1,0:T(8,128)(2,1)} %param.24) | copy-start | bytes 6291460
  7.2 125.9 %all-reduce.6.cloned.1.call-start = ((), (), s32[]{:S(2)}) async-start(), calls=%async_computation | async-start | bytes 393216 | tf_op jit(solution)/shard_map/psum | solution.py:71
  46.6 7.9 %copy-start.5 = (f32[24,4]{0,1:T(4,128)}, f32[24,4]{0,1:T(4,128)S(1)}, u32[]{:S(2)}) copy-start(f32[24,4]{0,1:T(4,128)S(1)} %get-tuple-element.88) | copy-start | bytes 1156
  54.5 2.7 %copy-start.1 = (f32[24,4,32,512]{3,2,1,0:T(8,128)}, f32[24,4,32,512]{3,2,1,0:T(8,128)S(1)}, u32[]{:S(2)}) copy-start(f32[24,4,32,512]{3,2,1,0:T(8,128)S(1)} %multiply_add_fusion) | copy-start | bytes 18874372
  57.2 78.0 %copy-start.2 = (bf16[24,4096]{1,0:T(8,128)(2,1)S(1)}, bf16[24,4096]{1,0:T(8,128)(2,1)}, u32[]{:S(2)}) copy-start(bf16[24,4096]{1,0:T(8,128)(2,1)} %param.18) | copy-start | bytes 589828
  57.2 78.0 %copy-start.3 = (f32[4096]{0:T(1024)S(1)}, f32[4096]{0:T(1024)}, u32[]{:S(2)}) copy-start(f32[4096]{0:T(1024)} %param.19) | copy-start | bytes 49156
  57.2 78.0 %copy-start.6 = (f32[4,64]{1,0:T(4,128)S(1)}, f32[4,64]{1,0:T(4,128)}, u32[]{:S(2)}) copy-start(f32[4,64]{1,0:T(4,128)} %param.27) | copy-start | bytes 3076
  57.2 82.5 %copy-start.8 = (u32[32]{0:T(128)S(1)}, u32[32]{0:T(128)}, u32[]{:S(2)}) copy-start(u32[32]{0:T(128)} %constant.57) | copy-start | bytes 388
  57.2 83.7 %copy-start.7 = (s32[24]{0:T(128)S(1)}, s32[24]{0:T(128)}, u32[]{:S(2)}) copy-start(s32[24]{0:T(128)} %param.33) | copy-start | bytes 292
  61.1 138.6 %all-gather.6.cloned.1.call-start = ((), (), s32[]{:S(2)}) async-start(), calls=%async_computation.1 | async-start | bytes 6684672 | tf_op jit(solution)/shard_map/all_gather | solution.py:84
  135.2 67.7 %copy-start.4 = (f32[4096]{0:T(1024)S(1)}, f32[4096]{0:T(1024)}, u32[]{:S(2)}) copy-start(f32[4096]{0:T(1024)} %param.28) | copy-start | bytes 49156
Sparse Core Ops, SparseCore 0:
  61.2 71.7 all-reduce.5
  139.2 60.4 all-gather.5
